TPU v7x, 128 devices: a whole 4x4x4 slice. The times are simulated.
128 devices in a mesh: row: 8 (over y, core), col: 16 (over x, z).
Axes of the slice: x: 4, y: 4, z: 4, core: 2. Of those that a mesh axis runs over, the one named last changes fastest.
Arguments:
- matrix_in: float32 [4, 4096, 2, 8192], P(None, 'row', None, 'col'), as said below
- panel_start: int32 [1], replicated, may hold values from 0 to 29
Outputs:
- matrix_out: float32 [4, 4096, 2, 8192], P(None, 'row', None, 'col')
Inputs may be any that keep to these rules, and one draw needn't show every extreme that they name: matrix_in is symmetric and positive definite.
All inputs are finite; a program needn't handle non-finite values.
Results may differ from a plain program's by a relative error of at most 0.0001.
Values sent between devices are 32-bit elements.
No kernel may reach another device: no remote copies, remote signals or barrier semaphores. Data moves between devices by JAX's collectives and lax.ppermute only.
A program may use at most 128 MiB of HBM per device.

v0:
```python
import jax
import jax.numpy as jnp
from jax import lax
from jax.experimental import pallas as pl
from jax.experimental.pallas import tpu as pltpu
from jax.sharding import PartitionSpec as P


F32 = jnp.float32
BF16 = jnp.bfloat16
T = 128
G = 8


def split2(x):
    hi = x.astype(BF16)
    return hi, (x - hi.astype(F32)).astype(BF16)


def split3(x):
    hi = x.astype(BF16)
    rest = x - hi.astype(F32)
    mid = rest.astype(BF16)
    return hi, mid, (rest - mid.astype(F32)).astype(BF16)


def dot(a, b, ca, cb):
    return lax.dot_general(a, b, (((ca,), (cb,)), ((), ())), preferred_element_type=F32)


def factor_block(block):
    groups = T // G
    sub = lax.broadcasted_iota(jnp.int32, (G, T), 0)
    lane = lax.broadcasted_iota(jnp.int32, (G, T), 1)
    upper = list(block)
    inv = [jnp.where(lane == sub + G * g, F32(1.0), F32(0.0)) for g in range(groups)]

    def over_lanes(x, i):
        return jnp.broadcast_to(x[:, i : i + 1], (G, T))

    def over_rows(x, i):
        return jnp.broadcast_to(x[i : i + 1, :], (G, T))

    ahead = [over_lanes(upper[0], i) for i in range(G)]
    for g in range(groups):
        a, w = upper[g], inv[g]
        cols = ahead
        scale, cross, rows_a, rows_w = [], {}, [], []
        for j in range(G):
            r = lax.rsqrt(over_rows(cols[j], j))
            scale.append(r)
            low = cols[j] * r
            for i in range(j + 1, G):
                cross[i, j] = over_rows(low, i)
                cols[i] = cols[i] - low * cross[i, j]
            u = over_rows(a, j) * r
            v = over_rows(w, j) * r
            rows_a.append(u)
            rows_w.append(v)
            below = jnp.where(sub > j, low, F32(0.0))
            a = jnp.where(sub == j, u, a - below * u)
            w = jnp.where(sub == j, v, w - below * v)
        upper[g], inv[g] = a, w
        for m in range(g + 1, groups):
            x, y = upper[m], inv[m]
            cols = [over_lanes(x, G * g + i) for i in range(G)]
            if m == g + 1:
                ahead = [over_lanes(x, G * m + i) for i in range(G)]
            for j in range(G):
                low = cols[j] * scale[j]
                for i in range(j + 1, G):
                    cols[i] = cols[i] - low * cross[i, j]
                if m == g + 1:
                    ahead = [p - low * over_rows(low, i) for i, p in enumerate(ahead)]
                x = x - low * rows_a[j]
                y = y - low * rows_w[j]
            upper[m], inv[m] = x, y
    return upper, inv


def prod6(a, b, ca, cb):
    (ah, am, al), (bh, bm, bl) = a, b
    acc = dot(ah, bl, ca, cb) + dot(al, bh, ca, cb) + dot(am, bm, ca, cb)
    acc = acc + (dot(ah, bm, ca, cb) + dot(am, bh, ca, cb))
    return acc + dot(ah, bh, ca, cb)


def prod3(a, b, ca, cb):
    (ah, al), (bh, bl) = a, b
    return dot(ah, bl, ca, cb) + dot(al, bh, ca, cb) + dot(ah, bh, ca, cb)


def chol_kernel(q_ref, own_ref, near_ref, u_ref, w_ref, d_ref, uh, um, ul):
    n = d_ref.shape[0]
    width = n // 2
    parts = (uh, um, ul)
    slab, lanes = width // 8, width // 2
    for ref, mine in ((own_ref, 0), (near_ref, 1)):
        for s in range(4):
            source = lax.rem(q_ref[0] - 2 * s + 8, 8)
            source = source + mine * (1 - 2 * lax.rem(source, 2))
            for e in range(2 * (slab // G)):
                rows = source * slab + (e // 2) * G
                for m in range(3):
                    dest = pl.ds(pl.multiple_of(rows + (m // 2) * width, G), G)
                    first = (m > 0) * width + (e % 2) * lanes
                    d_ref[dest, first : first + lanes] = ref[s, e * 3 + m]
    row = lax.broadcasted_iota(jnp.int32, (T, T), 0)
    col = lax.broadcasted_iota(jnp.int32, (T, T), 1)

    def body(b, carry):
        own = pl.ds(pl.multiple_of(b * T, T), T)
        for at in range(n // T):
            rest = slice(at * T, n)

            @pl.when(b == at)
            def _():
                strip = d_ref[rest.start : rest.start + T, rest]
                if at:
                    done = slice(0, at * T)
                    here = slice(at * T, at * T + T)
                    strip = strip - prod6(
                        [p[done, here] for p in parts], [p[done, rest] for p in parts], 0, 0
                    )
                u_ref[rest.start : rest.start + T, rest] = strip

        block = u_ref[own, own]
        upper, inv = factor_block([block[G * g : G * g + G, :] for g in range(T // G)])
        upper = jnp.where(col >= row, jnp.concatenate(upper, 0), F32(0.0))
        inv = jnp.concatenate(inv, 0)
        w_ref[own, :] = inv
        u_ref[own, own] = upper
        for p, x in zip(parts, split3(upper)):
            p[own, own] = x
        for at in range(n // T - 1):
            here = slice(at * T, at * T + T)
            rest = slice(at * T + T, n)

            @pl.when(b == at)
            def _():
                solved = prod6(split3(w_ref[here, :]), split3(u_ref[here, rest]), 1, 0)
                u_ref[here, rest] = solved
                for p, x in zip(parts, split3(solved)):
                    p[here, rest] = x

        return carry

    lax.fori_loop(0, n // T, body, 0)


def chol(q, mine, partner, width):
    n = 2 * width
    return pl.pallas_call(
        chol_kernel,
        grid_spec=pltpu.PrefetchScalarGridSpec(
            num_scalar_prefetch=1,
            grid=(1,),
            in_specs=[pl.BlockSpec(mine.shape, lambda g, f: (0, 0, 0, 0))] * 2,
            out_specs=[
                pl.BlockSpec((n, n), lambda g, f: (0, 0)),
                pl.BlockSpec((n, T), lambda g, f: (0, 0)),
            ],
            scratch_shapes=[pltpu.VMEM((n, n), F32)] + [pltpu.VMEM((n, n), BF16)] * 3,
        ),
        out_shape=(jax.ShapeDtypeStruct((n, n), F32), jax.ShapeDtypeStruct((n, T), F32)),
        compiler_params=pltpu.CompilerParams(vmem_limit_bytes=48 * 2**20),
        name="chol",
    )(q, mine, partner)


def strip_kernel(at_ref, first_ref, second_ref, x_ref, *cand_refs):
    width = x_ref.shape[0] // 2
    lanes = width // T
    for p, ref in enumerate((first_ref, second_ref)):
        keep = at_ref[2 + p] > 0
        for j in range(2):
            for t in range(lanes):
                value = ref[pl.ds(t * 2 + j, width, stride=2 * lanes), :]
                cols = slice(j * width + t * T, j * width + t * T + T)
                x_ref[p * width : p * width + width, cols] = jnp.where(keep, value, F32(0.0))
    rows = cand_refs[0].shape[0]
    cols = pl.ds(pl.multiple_of(at_ref[5] * width, width), width)
    for s, ref in enumerate(cand_refs):
        chunk = lax.rem(at_ref[6] + s, len(cand_refs))
        ref[...] = x_ref[pl.ds(pl.multiple_of(at_ref[4] * width + chunk * rows, rows), rows), cols]


def strips(at, flat, width, rows_dev):
    per = width * 2 * (width // T)
    n = 2 * width
    piece = width // rows_dev
    flat = pltpu.with_memory_space_constraint(flat, pltpu.HBM)
    return pl.pallas_call(
        strip_kernel,
        grid_spec=pltpu.PrefetchScalarGridSpec(
            num_scalar_prefetch=1,
            grid=(1,),
            in_specs=[
                pl.BlockSpec((per, T), lambda g, f: (f[0], 0)),
                pl.BlockSpec((per, T), lambda g, f: (f[1], 0)),
            ],
            out_specs=[pl.BlockSpec((n, n), lambda g, f: (0, 0))]
            + [pl.BlockSpec((piece, width), lambda g, f: (0, 0))] * rows_dev,
        ),
        out_shape=[jax.ShapeDtypeStruct((n, n), F32)]
        + [jax.ShapeDtypeStruct((piece, width), F32)] * rows_dev,
        compiler_params=pltpu.CompilerParams(vmem_limit_bytes=40 * 2**20),
        name="strips",
    )(at, flat, flat)


def finish_kernel(
    flag_ref, mode_ref, u_ref, w_ref, r_ref, own_ref, other_ref, a_ref, o_ref,
    uh, ul, wh, wl, rest_ref, rh, rl, ch, cl, c_ref, sems,
):
    n = u_ref.shape[0]
    width = n // 2
    wide = 2 * T
    lanes = width // T
    step = pl.program_id(0)
    q = flag_ref[6, 0]

    def slab_copy(s):
        source = lax.rem(q - 2 * (s // 2) + 8, 8)
        if s % 2:
            source = source + 1 - 2 * lax.rem(source, 2)
        rows = pl.ds(pl.multiple_of(source * T, T), T)
        ref = (own_ref, other_ref)[s % 2]
        return pltpu.make_async_copy(ref.at[s // 2], c_ref.at[rows, :], sems.at[s])

    @pl.when(step == 0)
    def _():
        for s in range(8):
            slab_copy(s).start()
        uh[...], ul[...] = split2(u_ref[...])
        for b in range(n // wide):
            r0 = slice(b * wide, b * wide + T)
            r1 = slice(b * wide + T, b * wide + wide)
            w0, w1 = split3(w_ref[r0, :]), split3(w_ref[r1, :])
            cross = prod6(split3(u_ref[r0, r1]), w0, 0, 0)
            corner = -prod6(w1, split3(cross), 1, 0)
            zero = jnp.zeros((T, T), F32)
            top = jnp.concatenate([w_ref[r0, :], zero], 1)
            low = jnp.concatenate([corner, w_ref[r1, :]], 1)
            wh[b * wide : b * wide + wide, :], wl[b * wide : b * wide + wide, :] = split2(
                jnp.concatenate([top, low], 0)
            )

    def solve(b_ref, hi_ref, lo_ref, base, slot, at, size):
        cols = pl.ds(at, size)
        for b in range(n // wide):
            own = slice(b * wide, b * wide + wide)
            rest = slice(b * wide + wide, n)
            src = rest_ref if b else b_ref
            sol = split2(prod3((wh[own, :], wl[own, :]), split2(src[own, cols]), 1, 0))
            for ref, x in zip((hi_ref, lo_ref), sol):
                for e in range(size // width):
                    keep = flag_ref[base + slot + e, b * wide // width] > 0
                    piece = x[:, e * width : e * width + width]
                    where = pl.ds(pl.multiple_of((slot + e) * width, width), width)
                    ref[own, where] = jnp.where(keep, piece, jnp.zeros_like(piece))
            if rest.start < n:
                rest_ref[rest, cols] = src[rest, cols] - prod3((uh[own, rest], ul[own, rest]), sol, 0, 0)

    def solve_pair(b_ref, hi_ref, lo_ref, base, slot):
        first, second = flag_ref[base + slot, 0], flag_ref[base + slot + 1, 0]

        @pl.when(first + second == 2)
        def _():
            solve(b_ref, hi_ref, lo_ref, base, slot, 0, 2 * width)

        @pl.when(first + second == 1)
        def _():
            at = pl.multiple_of(second * width, width)
            solve(b_ref, hi_ref, lo_ref, base, slot + second, at, width)

    @pl.when(step < 2)
    def _():
        solve_pair(r_ref, rh, rl, 0, 2 * step)

    @pl.when(step == 2)
    def _():
        for s in range(8):
            slab_copy(s).wait()
        solve_pair(c_ref, ch, cl, 4, 0)

    @pl.when(step >= 3)
    def _():
        block = step - 3
        mine = pl.ds(pl.multiple_of((lax.rem(block, 2) * 2 + block // 2) * width, width), width)

        def put(j, value, keep):
            for t in range(lanes):
                at = pl.ds(t * 2 + j, width, stride=2 * lanes)
                piece = value[:, t * T : t * T + T]
                o_ref[at, :] = a_ref[at, :] - piece if keep else piece

        def product(cols):
            return prod3((rh[:, mine], rl[:, mine]), (ch[:, cols], cl[:, cols]), 0, 0)

        both = (mode_ref[block, 0] == 0) & (mode_ref[block, 1] == 0)

        @pl.when(both)
        def _():
            value = product(slice(0, 2 * width))
            for j in range(2):
                put(j, value[:, j * width : j * width + width], True)

        @pl.when(jnp.logical_not(both))
        def _():
            def column(j, carry):
                mode = mode_ref[block, j]

                @pl.when(mode == 0)
                def _():
                    put(j, product(pl.ds(pl.multiple_of(j * width, width), width)), True)

                @pl.when(mode == 5)
                def _():
                    for t in range(lanes):
                        at = pl.ds(t * 2 + j, width, stride=2 * lanes)
                        o_ref[at, :] = a_ref[at, :]

                panel = pl.multiple_of(lax.rem(mode + 1, 2) * width, width)
                rows = pl.ds(panel, width)

                @pl.when((mode == 1) | (mode == 2))
                def _():
                    put(j, (rh[rows, mine].astype(F32) + rl[rows, mine].astype(F32)).T, False)

                @pl.when((mode == 3) | (mode == 4))
                def _():
                    tri = u_ref[rows, rows]
                    r = lax.broadcasted_iota(jnp.int32, tri.shape, 0)
                    s = lax.broadcasted_iota(jnp.int32, tri.shape, 1)
                    put(j, jnp.where(s >= r, tri, F32(0.0)).T, False)

                return carry

            lax.fori_loop(0, 2, column, 0)


def finish(flags, modes, u, w, rpart, own, other, flat):
    n = u.shape[0]
    width = n // 2
    per = width * 2 * (width // T)
    loc_rows = flat.shape[0] // per
    once = pl.Buffered(1)

    def block(t, f, m):
        return (jnp.maximum(t - 3, 0), 0)

    return pl.pallas_call(
        finish_kernel,
        grid_spec=pltpu.PrefetchScalarGridSpec(
            num_scalar_prefetch=2,
            grid=(3 + loc_rows,),
            in_specs=[
                pl.BlockSpec((n, n), lambda t, f, m: (0, 0), pipeline_mode=once),
                pl.BlockSpec((n, T), lambda t, f, m: (0, 0), pipeline_mode=once),
                pl.BlockSpec((n, n), lambda t, f, m: (0, jnp.minimum(t, 1))),
            ]
            + [pl.BlockSpec(memory_space=pl.ANY)] * 2
            + [pl.BlockSpec((per, T), block)],
            out_specs=pl.BlockSpec((per, T), block),
            scratch_shapes=[pltpu.VMEM((n, n), BF16)] * 2
            + [pltpu.VMEM((n, 2 * T), BF16)] * 2
            + [pltpu.VMEM((n, n), F32)]
            + [pltpu.VMEM((n, 2 * n), BF16)] * 2
            + [pltpu.VMEM((n, n), BF16)] * 2
            + [pltpu.VMEM((n, n), F32), pltpu.SemaphoreType.DMA((8,))],
        ),
        out_shape=jax.ShapeDtypeStruct(flat.shape, F32),
        compiler_params=pltpu.CompilerParams(vmem_limit_bytes=58 * 2**20),
        name="finish",
    )(flags, modes, u, w, rpart, own, other, flat)


def diagonal(chunks, k, q, c, rows_dev, cols_dev, width):
    oc = k % cols_dev
    home = c % rows_dev
    recv = [chunks[0]]
    for s in range(1, rows_dev):
        pairs = [(r, (r + s) % rows_dev) for r in range(rows_dev)]
        recv.append(lax.ppermute(chunks[s], "row", pairs))
    diag, upper = recv[0], recv[0]
    for s in range(1, rows_dev):
        diag = jnp.where((q - home) % rows_dev == s, recv[s], diag)
        upper = jnp.where((q - home + 1) % rows_dev == s, recv[s], upper)
    slots = jnp.stack([jnp.where(c == oc, diag, upper), diag])
    rows = slots.shape[1]
    slots = slots.reshape(2, rows // G, G, 2, width // 2).transpose(1, 3, 0, 2, 4)
    got = lax.all_to_all(slots.reshape(cols_dev, 2, G, width // 2), "col", 0, 0)

    return got


def gathered_over_cols(got, k, cols_dev):
    oc, oc1 = k % cols_dev, (k + 1) % cols_dev

    def pick(p, slot):
        return lax.dynamic_index_in_dim(got, p, 0, keepdims=False)[slot]

    d = jnp.concatenate([pick(oc, 0), pick(oc1, 0), pick(oc1, 1)], 0)
    return lax.all_gather(d, "col", axis=0, tiled=True)


def over_rows_of_devices(d, rows_dev, width):
    parts = [d]
    for s in range(1, rows_dev // 2):
        pairs = [(r, (r + 2 * s) % rows_dev) for r in range(rows_dev)]
        parts.append(lax.ppermute(d, "row", pairs))
    mine = jnp.stack(parts).reshape(len(parts), -1, G, width // 2)
    partner = lax.ppermute(mine, "row", [(r, r ^ 1) for r in range(rows_dev)])
    return mine, partner


def per_device(matrix, panel_start):
    rows_dev, cols_dev = lax.axis_size("row"), lax.axis_size("col")
    q, c = lax.axis_index("row"), lax.axis_index("col")
    loc_rows, width, loc_cols, _ = matrix.shape
    both = ("row", "col")
    k = panel_start[0]
    k1 = k + 1

    lanes = width // T
    flat = matrix.reshape(loc_rows, width, loc_cols, lanes, T).transpose(0, 1, 3, 2, 4)
    flat = flat.reshape(-1, T)
    oc = k % cols_dev
    diag_here = q == c % rows_dev
    at = jnp.stack(
        [
            k // rows_dev,
            k1 // rows_dev,
            (q == k % rows_dev).astype(jnp.int32),
            (q == k1 % rows_dev).astype(jnp.int32),
            jnp.where(diag_here & (c != oc), 1, 0),
            jnp.where(diag_here & (c == oc), k // cols_dev, k1 // cols_dev),
            q,
        ]
    ).astype(jnp.int32)
    x, *chunks = strips(at, flat, width, rows_dev)
    y = lax.psum_scatter(x, "row", scatter_dimension=0, tiled=True)
    piece = y.shape[0]
    half = piece // 2

    got = diagonal(chunks, k, q, c, rows_dev, cols_dev, width)
    got, y = lax.optimization_barrier((got, y))

    late = c >= rows_dev
    send = (
        jnp.where(late, y[half:], y[:half]),
        jnp.where(late, y[:half], y[half:]),
    )
    recv = []
    for h in range(2):
        pairs = []
        for r in range(rows_dev):
            for s in range(cols_dev):
                flip = h if s < rows_dev else 1 - h
                pairs.append((r * cols_dev + s, (s % rows_dev) * cols_dev + 2 * r + flip))
        recv.append(lax.ppermute(send[h], both, pairs))

    even = c % 2 == 0
    z = jnp.concatenate(
        [jnp.where(even, recv[0], recv[1]), jnp.where(even, recv[1], recv[0])], 1
    )
    rpart = lax.all_gather(z, "col", axis=0, tiled=True)
    own = [y]
    for s in range(1, rows_dev // 2):
        pairs = [(r, (r + 2 * s) % rows_dev) for r in range(rows_dev)]
        own.append(lax.ppermute(y, "row", pairs))
    got, z = lax.optimization_barrier((got, z))
    d = gathered_over_cols(got, k, cols_dev)
    mine, partner = over_rows_of_devices(d, rows_dev, width)
    own = jnp.stack(own)
    mine, partner, own = lax.optimization_barrier((mine, partner, own))
    other = lax.ppermute(own, "row", [(r, r ^ 1) for r in range(rows_dev)])
    u, w = chol(q.astype(jnp.int32)[None], mine, partner, width)

    i = jnp.arange(loc_rows, dtype=jnp.int32)
    slot_rows = ((i // 2) + 2 * (i % 2)) * rows_dev + q
    glob_cols = jnp.arange(loc_cols, dtype=jnp.int32) * cols_dev + c
    panels = jnp.stack([k, k1])
    flags_r = (slot_rows[:, None] > panels[None, :]).astype(jnp.int32)
    flags_c = (glob_cols[:, None] > panels[None, :]).astype(jnp.int32)
    chip = jnp.stack([q, q])[None].astype(jnp.int32)
    flags = jnp.concatenate([flags_r, flags_c, chip], 0)

    gr = (i * rows_dev + q)[:, None]
    gc = glob_cols[None, :]
    modes = jnp.where(
        gc == k,
        jnp.where(gr > k, 1, jnp.where(gr == k, 3, 5)),
        jnp.where(
            gc == k1,
            jnp.where(gr > k1, 2, jnp.where(gr == k1, 4, 5)),
            jnp.where((gr > k) & (gc > k), 0, 5),
        ),
    ).astype(jnp.int32)
    out = finish(flags, modes, u, w, rpart, own, other, flat)
    out = out.reshape(loc_rows, width, lanes, loc_cols, T).transpose(0, 1, 3, 2, 4)
    return out.reshape(matrix.shape)


def solution(mesh):
    return jax.shard_map(
        per_device,
        mesh=mesh,
        in_specs=(P(None, "row", None, "col"), P()),
        out_specs=P(None, "row", None, "col"),
        check_vma=False,
    )
```

profile of v0, /device:TPU:31, one launch (start us, length us, event | category | flops | bytes accessed | tf_op | source)
XLA Modules:
  0.0 225.0 jit_solution(9958778082782422024)
XLA Ops:
  6.5 0.0 reduce-scatter.2.cloned.1.call-start
  7.3 0.1 stack.92.at_ref
  7.4 4.4 %strips.1 = (f32[1024,1024]{1,0:T(8,128)S(1)}, f32[64,512]{1,0:T(8,128)S(1)}, f32[64,512]{1,0:T(8,128)S(1)}, f32[64,512]{1,0:T(8,128)S(1)}, f32[64,512]{1,0:T(8,...) custom-call(s32[7]{0:T(128)S(1)} %stack.92.at_ref, ...), custom_call_target="tpu_custom_call" | custom-call | tf_op jit(solution)/shard_map/strips/pallas_call | solution.py:193
  11.8 0.0 copy-start
  11.9 2.0 copy-done
  13.9 0.0 reduce-scatter.2.cloned.1.call-update
  13.9 0.7 collective-permute-start
  14.6 0.5 collective-permute-start.1
  15.0 0.4 collective-permute-start.2
  15.4 3.3 %collective-permute-start.3 = (f32[64,512]{1,0:T(8,128)S(1)}, f32[64,512]{1,0:T(8,128)S(1)}, u32[]{:S(2)}, u32[]{:S(2)}) collective-permute-start(f32[64,512]{1,0:T(8,128)S(1)} %get-tuple-element.25), channel_id=1, source_target_pairs={{0,64},{16,80},{32,96},{48,112},{64,0},{80,16},{96,32},{112,48},{1... | collective-permute-start | bytes 393224 | tf_op jit(solution)/shard_map/ppermute | solution.py:385
  18.8 0.4 collective-permute-start.4
  19.2 1.6 collective-permute-done
  20.8 0.3 collective-permute-start.5
  21.1 0.2 collective-permute-done.1
  21.3 8.0 %collective-permute-start.6 = (f32[64,512]{1,0:T(8,128)S(1)}, f32[64,512]{1,0:T(8,128)S(1)}, u32[]{:S(2)}, u32[]{:S(2)}) collective-permute-start(f32[64,512]{1,0:T(8,128)S(1)} %get-tuple-element.28), channel_id=1, source_target_pairs={{0,16},{16,32},{32,48},{48,64},{64,80},{80,96},{96,112},{112,0},{1... | collective-permute-start | bytes 393224 | tf_op jit(solution)/shard_map/ppermute | solution.py:385
  29.3 0.0 collective-permute-done.2
  29.3 0.0 collective-permute-done.3
  29.3 0.0 collective-permute-done.4
  29.3 0.1 collective-permute-done.5
  29.4 3.8 %collective-permute-done.6 = f32[64,512]{1,0:T(8,128)S(1)} collective-permute-done((f32[64,512]{1,0:T(8,128)S(1)}, f32[64,512]{1,0:T(8,128)S(1)}, u32[]{:S(2)}, u32[]{:S(2)}) %collective-permute-start.6) | collective-permute-done | bytes 131104 | tf_op jit(solution)/shard_map/ppermute | solution.py:385
  33.2 0.1 select_select_fusion.1
  33.3 0.1 select_select_fusion
  33.4 0.7 copy.12
  34.1 7.8 %all-to-all-start = ((f32[16,2,8,256]{3,2,1,0:T(8,128)}), f32[16,2,8,256]{3,2,1,0:T(8,128)S(1)}, u32[]{:S(2)}, u32[]{:S(2)}) async-start(f32[16,2,8,256]{3,2,1,0:T(8,128)} %bitcast.16), calls=%async_computation | async-start | bytes 524288 | tf_op jit(solution)/shard_map/all_to_all | solution.py:393
  42.0 0.0 all-gather.2.cloned.1.call-start
  42.0 5.5 %all-to-all-done = f32[16,2,8,256]{3,2,1,0:T(8,128)S(1)} async-done(((f32[16,2,8,256]{3,2,1,0:T(8,128)}), f32[16,2,8,256]{3,2,1,0:T(8,128)S(1)}, u32[]{:S(2)}, u32[]{:S(2)}) %all-to-all-start) | async-done | bytes 262176 | tf_op jit(solution)/shard_map/all_to_all | solution.py:393
  47.5 10.2 %reduce-scatter.2.cloned.1.call-done = f32[128,1024]{1,0:T(8,128)} async-done(((f32[1024,1024]{1,0:T(8,128)}), f32[128,1024]{1,0:T(8,128)}) %reduce-scatter.2.cloned.1.call-update) | async-done | bytes 524304 | tf_op jit(solution)/shard_map/reduce_scatter | solution.py:443
  57.7 1.1 slice_select_fusion.1
  58.8 3.1 %collective-permute-start.7 = (f32[64,1024]{1,0:T(8,128)S(1)}, f32[64,1024]{1,0:T(8,128)S(1)}, u32[]{:S(2)}, u32[]{:S(2)}) collective-permute-start(f32[64,1024]{1,0:T(8,128)S(1)} %get-tuple-element.41), channel_id=1, source_target_pairs={{0,0},{1,16},{2,32},{3,48},{4,64},{5,80},{6,96},{7,112},{8,1},{9,1... | collective-permute-start | bytes 786440 | tf_op jit(solution)/shard_map/ppermute | solution.py:462
  61.9 1.5 collective-permute-start.8
  63.4 16.7 %collective-permute-done.7 = f32[64,1024]{1,0:T(8,128)S(1)} collective-permute-done((f32[64,1024]{1,0:T(8,128)S(1)}, f32[64,1024]{1,0:T(8,128)S(1)}, u32[]{:S(2)}, u32[]{:S(2)}) %collective-permute-start.7) | collective-permute-done | bytes 262176 | tf_op jit(solution)/shard_map/ppermute | solution.py:462
  80.1 4.5 %collective-permute-done.8 = f32[64,1024]{1,0:T(8,128)S(1)} collective-permute-done((f32[64,1024]{1,0:T(8,128)S(1)}, f32[64,1024]{1,0:T(8,128)S(1)}, u32[]{:S(2)}, u32[]{:S(2)}) %collective-permute-start.8) | collective-permute-done | bytes 262176 | tf_op jit(solution)/shard_map/ppermute | solution.py:462
  84.6 0.8 pad_maximum_fusion.2
  85.4 0.0 all-gather.2.cloned.1.call-update
  85.5 23.4 %all_gather.6 = f32[384,256]{1,0:T(8,128)S(1)} all-gather(f32[24,256]{1,0:T(8,128)S(1)} %pad_maximum_fusion.3), channel_id=1, replica_groups=mesh['row'=8,'col'=16] {'col'}, dimensions={0}, use_global_device_ids=true | all-gather | bytes 417792 | tf_op jit(solution)/shard_map/all_gather | solution.py:405
  108.9 0.0 collective-permute-start.11
  108.9 1.9 collective-permute-start.10
  110.8 0.8 collective-permute-start.9
  111.6 10.4 %collective-permute-done.11 = f32[384,256]{1,0:T(8,128)S(1)} collective-permute-done((f32[384,256]{1,0:T(8,128)S(1)}, f32[384,256]{1,0:T(8,128)S(1)}, u32[]{:S(2)}, u32[]{:S(2)}) %collective-permute-start.11) | collective-permute-done | bytes 393248 | tf_op jit(solution)/shard_map/ppermute | solution.py:412
  122.0 0.0 collective-permute-done.10
  122.0 4.1 %collective-permute-done.9 = f32[384,256]{1,0:T(8,128)S(1)} collective-permute-done((f32[384,256]{1,0:T(8,128)S(1)}, f32[384,256]{1,0:T(8,128)S(1)}, u32[]{:S(2)}, u32[]{:S(2)}) %collective-permute-start.9) | collective-permute-done | bytes 393248 | tf_op jit(solution)/shard_map/ppermute | solution.py:412
  126.1 0.1 pad_maximum_fusion.1.own_ref
  126.2 4.7 %collective-permute-start.12 = (f32[4,48,8,256]{3,2,1,0:T(8,128)S(1)}, f32[4,48,8,256]{3,2,1,0:T(8,128)S(1)}, u32[]{:S(2)}, u32[]{:S(2)}) collective-permute-start(f32[4,48,8,256]{3,2,1,0:T(8,128)S(1)} %pad_maximum_fusion.1.own_ref), channel_id=1, source_target_pairs={{0,16},{16,0},{32,48},{48,32},{64,80},{80,64},{96,112},{112,96},{1... | collective-permute-start | bytes 4718600 | tf_op jit(solution)/shard_map/ppermute | solution.py:414
  130.9 0.0 copy-done.3
  130.9 0.6 collective-permute-start.14
  131.5 1.7 collective-permute-start.13
  133.2 0.3 collective-permute-start.15
  133.5 12.3 %collective-permute-done.14 = f32[128,1024]{1,0:T(8,128)S(1)} collective-permute-done((f32[128,1024]{1,0:T(8,128)S(1)}, f32[128,1024]{1,0:T(8,128)S(1)}, u32[]{:S(2)}, u32[]{:S(2)}) %collective-permute-start.14) | collective-permute-done | bytes 524320 | tf_op jit(solution)/shard_map/ppermute | solution.py:472
  145.9 11.0 %collective-permute-done.13 = f32[128,1024]{1,0:T(8,128)S(1)} collective-permute-done((f32[128,1024]{1,0:T(8,128)S(1)}, f32[128,1024]{1,0:T(8,128)S(1)}, u32[]{:S(2)}, u32[]{:S(2)}) %collective-permute-start.13) | collective-permute-done | bytes 524320 | tf_op jit(solution)/shard_map/ppermute | solution.py:472
  156.8 0.8 collective-permute-done.15
  157.6 0.2 pad_maximum_fusion.own_ref
  157.8 0.0 copy-start.2
  157.8 0.0 collective-permute-done.12.near_ref
  157.8 0.6 collective-permute-start.16
  158.5 0.1 add_bitcast_fusion
  158.5 0.1 pad_add_fusion.1
  158.6 0.1 compare_convert_fusion
  158.7 0.1 compare_convert_fusion.1
  158.8 0.6 pad_add_fusion.flag_ref
  159.4 0.7 select_select_fusion.2.mode_ref
  160.0 32.8 %chol.1 = (f32[1024,1024]{1,0:T(8,128)}, f32[1024,128]{1,0:T(8,128)S(1)}) custom-call(s32[1]{0:T(128)} %bitcast.2.q_ref, f32[4,48,8,256]{3,2,1,0:T(8,128)S(1)} %pad_maximum_fusion.1.own_ref, f32[4,48,8,256]{3,2,1,0:T(8,128)S(1)} %collective-permute-done.12.near_ref), custom_call_target="tpu_custom_call" | custom-call | tf_op jit(solution)/shard_map/chol/pallas_call | solution.py:153
  192.8 0.8 copy-done.1
  193.6 0.0 collective-permute-done.16.other_ref
  193.6 24.6 %finish.1 = f32[16384,128]{1,0:T(8,128)} custom-call(s32[7,2]{1,0:T(8,128)} %pad_add_fusion.flag_ref, s32[4,2]{1,0:T(4,128)} %select_select_fusion.2.mode_ref, f32[1024,1024]{1,0:T(8,128)} %get-tuple-element.36.u_ref, f32[1024,128]{1,0:T(8,128)} %copy-done.1, f32[1024,2048]{1,0:T(8,128)} %all-gather.2.cloned.1.call-done.r_ref, f32[4,128,1024]{2,1,0:T(8,128)} %copy-done.2, ...), custom_call_target="tpu_custom_call" | custom-call | tf_op jit(solution)/shard_map/finish/pallas_call | solution.py:353
  (13 shorter events, 0.1 us)
Async XLA Ops:
  6.5 51.2 %reduce-scatter.2.cloned.1.call-start = ((), (), s32[]{:S(2)}) async-start(), calls=%async_computation.2 | async-start | bytes 4718592 | tf_op jit(solution)/shard_map/reduce_scatter | solution.py:443
  11.8 2.0 copy-start
  13.9 6.9 %collective-permute-start = (f32[64,512]{1,0:T(8,128)S(1)}, f32[64,512]{1,0:T(8,128)S(1)}, u32[]{:S(2)}, u32[]{:S(2)}) collective-permute-start(f32[64,512]{1,0:T(8,128)S(1)} %get-tuple-element.22), channel_id=1, source_target_pairs={{0,112},{16,0},{32,16},{48,32},{64,48},{80,64},{96,80},{112,96},{1... | collective-permute-start | bytes 393224 | tf_op jit(solution)/shard_map/ppermute | solution.py:385
  14.6 6.7 %collective-permute-start.1 = (f32[64,512]{1,0:T(8,128)S(1)}, f32[64,512]{1,0:T(8,128)S(1)}, u32[]{:S(2)}, u32[]{:S(2)}) collective-permute-start(f32[64,512]{1,0:T(8,128)S(1)} %get-tuple-element.23), channel_id=1, source_target_pairs={{0,96},{16,112},{32,0},{48,16},{64,32},{80,48},{96,64},{112,80},{1... | collective-permute-start | bytes 393224 | tf_op jit(solution)/shard_map/ppermute | solution.py:385
  15.0 14.3 %collective-permute-start.2 = (f32[64,512]{1,0:T(8,128)S(1)}, f32[64,512]{1,0:T(8,128)S(1)}, u32[]{:S(2)}, u32[]{:S(2)}) collective-permute-start(f32[64,512]{1,0:T(8,128)S(1)} %get-tuple-element.24), channel_id=1, source_target_pairs={{0,80},{16,96},{32,112},{48,0},{64,16},{80,32},{96,48},{112,64},{1... | collective-permute-start | bytes 393224 | tf_op jit(solution)/shard_map/ppermute | solution.py:385
  15.4 13.9 %collective-permute-start.3 = (f32[64,512]{1,0:T(8,128)S(1)}, f32[64,512]{1,0:T(8,128)S(1)}, u32[]{:S(2)}, u32[]{:S(2)}) collective-permute-start(f32[64,512]{1,0:T(8,128)S(1)} %get-tuple-element.25), channel_id=1, source_target_pairs={{0,64},{16,80},{32,96},{48,112},{64,0},{80,16},{96,32},{112,48},{1... | collective-permute-start | bytes 393224 | tf_op jit(solution)/shard_map/ppermute | solution.py:385
  18.8 10.5 %collective-permute-start.4 = (f32[64,512]{1,0:T(8,128)S(1)}, f32[64,512]{1,0:T(8,128)S(1)}, u32[]{:S(2)}, u32[]{:S(2)}) collective-permute-start(f32[64,512]{1,0:T(8,128)S(1)} %get-tuple-element.26), channel_id=1, source_target_pairs={{0,48},{16,64},{32,80},{48,96},{64,112},{80,0},{96,16},{112,32},{1... | collective-permute-start | bytes 393224 | tf_op jit(solution)/shard_map/ppermute | solution.py:385
  20.8 8.6 %collective-permute-start.5 = (f32[64,512]{1,0:T(8,128)S(1)}, f32[64,512]{1,0:T(8,128)S(1)}, u32[]{:S(2)}, u32[]{:S(2)}) collective-permute-start(f32[64,512]{1,0:T(8,128)S(1)} %get-tuple-element.27), channel_id=1, source_target_pairs={{0,32},{16,48},{32,64},{48,80},{64,96},{80,112},{96,0},{112,16},{1... | collective-permute-start | bytes 393224 | tf_op jit(solution)/shard_map/ppermute | solution.py:385
  21.3 11.9 %collective-permute-start.6 = (f32[64,512]{1,0:T(8,128)S(1)}, f32[64,512]{1,0:T(8,128)S(1)}, u32[]{:S(2)}, u32[]{:S(2)}) collective-permute-start(f32[64,512]{1,0:T(8,128)S(1)} %get-tuple-element.28), channel_id=1, source_target_pairs={{0,16},{16,32},{32,48},{48,64},{64,80},{80,96},{96,112},{112,0},{1... | collective-permute-start | bytes 393224 | tf_op jit(solution)/shard_map/ppermute | solution.py:385
  34.1 13.4 %all-to-all-start = ((f32[16,2,8,256]{3,2,1,0:T(8,128)}), f32[16,2,8,256]{3,2,1,0:T(8,128)S(1)}, u32[]{:S(2)}, u32[]{:S(2)}) async-start(f32[16,2,8,256]{3,2,1,0:T(8,128)} %bitcast.16), calls=%async_computation | async-start | bytes 524288 | tf_op jit(solution)/shard_map/all_to_all | solution.py:393
  42.0 151.6 %all-gather.2.cloned.1.call-start = ((), (), s32[]{:S(2)}) async-start(), calls=%async_computation.3 | async-start | bytes 8912896 | tf_op jit(solution)/shard_map/all_gather | solution.py:468
  58.8 21.3 %collective-permute-start.7 = (f32[64,1024]{1,0:T(8,128)S(1)}, f32[64,1024]{1,0:T(8,128)S(1)}, u32[]{:S(2)}, u32[]{:S(2)}) collective-permute-start(f32[64,1024]{1,0:T(8,128)S(1)} %get-tuple-element.41), channel_id=1, source_target_pairs={{0,0},{1,16},{2,32},{3,48},{4,64},{5,80},{6,96},{7,112},{8,1},{9,1... | collective-permute-start | bytes 786440 | tf_op jit(solution)/shard_map/ppermute | solution.py:462
  61.9 22.7 %collective-permute-start.8 = (f32[64,1024]{1,0:T(8,128)S(1)}, f32[64,1024]{1,0:T(8,128)S(1)}, u32[]{:S(2)}, u32[]{:S(2)}) collective-permute-start(f32[64,1024]{1,0:T(8,128)S(1)} %get-tuple-element.42), channel_id=1, source_target_pairs={{0,1},{1,17},{2,33},{3,49},{4,65},{5,81},{6,97},{7,113},{8,0},{9,1... | collective-permute-start | bytes 786440 | tf_op jit(solution)/shard_map/ppermute | solution.py:462
  85.4 45.5 %copy-start.3 = (f32[128,1024]{1,0:T(8,128)S(1)}, f32[128,1024]{1,0:T(8,128)}, u32[]{:S(2)}) copy-start(f32[128,1024]{1,0:T(8,128)} %reduce-scatter.2.cloned.1.call-done) | copy-start | bytes 1572868
  108.9 13.1 %collective-permute-start.11 = (f32[384,256]{1,0:T(8,128)S(1)}, f32[384,256]{1,0:T(8,128)S(1)}, u32[]{:S(2)}, u32[]{:S(2)}) collective-permute-start(f32[384,256]{1,0:T(8,128)S(1)} %all_gather.6), channel_id=1, source_target_pairs={{0,96},{16,112},{32,0},{48,16},{64,32},{80,48},{96,64},{112,80},{1... | collective-permute-start | bytes 1179656 | tf_op jit(solution)/shard_map/ppermute | solution.py:412
  108.9 13.1 %collective-permute-start.10 = (f32[384,256]{1,0:T(8,128)S(1)}, f32[384,256]{1,0:T(8,128)S(1)}, u32[]{:S(2)}, u32[]{:S(2)}) collective-permute-start(f32[384,256]{1,0:T(8,128)S(1)} %all_gather.6), channel_id=1, source_target_pairs={{0,64},{16,80},{32,96},{48,112},{64,0},{80,16},{96,32},{112,48},{1... | collective-permute-start | bytes 1179656 | tf_op jit(solution)/shard_map/ppermute | solution.py:412
  110.8 15.3 %collective-permute-start.9 = (f32[384,256]{1,0:T(8,128)S(1)}, f32[384,256]{1,0:T(8,128)S(1)}, u32[]{:S(2)}, u32[]{:S(2)}) collective-permute-start(f32[384,256]{1,0:T(8,128)S(1)} %all_gather.6), channel_id=1, source_target_pairs={{0,32},{16,48},{32,64},{48,80},{64,96},{80,112},{96,0},{112,16},{1... | collective-permute-start | bytes 1179656 | tf_op jit(solution)/shard_map/ppermute | solution.py:412
  126.2 31.6 %collective-permute-start.12 = (f32[4,48,8,256]{3,2,1,0:T(8,128)S(1)}, f32[4,48,8,256]{3,2,1,0:T(8,128)S(1)}, u32[]{:S(2)}, u32[]{:S(2)}) collective-permute-start(f32[4,48,8,256]{3,2,1,0:T(8,128)S(1)} %pad_maximum_fusion.1.own_ref), channel_id=1, source_target_pairs={{0,16},{16,0},{32,48},{48,32},{64,80},{80,64},{96,112},{112,96},{1... | collective-permute-start | bytes 4718600 | tf_op jit(solution)/shard_map/ppermute | solution.py:414
  130.9 14.9 %collective-permute-start.14 = (f32[128,1024]{1,0:T(8,128)S(1)}, f32[128,1024]{1,0:T(8,128)S(1)}, u32[]{:S(2)}, u32[]{:S(2)}) collective-permute-start(f32[128,1024]{1,0:T(8,128)S(1)} %copy-done.3), channel_id=1, source_target_pairs={{0,64},{16,80},{32,96},{48,112},{64,0},{80,16},{96,32},{112,48},{1... | collective-permute-start | bytes 1572872 | tf_op jit(solution)/shard_map/ppermute | solution.py:472
  131.5 25.3 %collective-permute-start.13 = (f32[128,1024]{1,0:T(8,128)S(1)}, f32[128,1024]{1,0:T(8,128)S(1)}, u32[]{:S(2)}, u32[]{:S(2)}) collective-permute-start(f32[128,1024]{1,0:T(8,128)S(1)} %copy-done.3), channel_id=1, source_target_pairs={{0,32},{16,48},{32,64},{48,80},{64,96},{80,112},{96,0},{112,16},{1... | collective-permute-start | bytes 1572872 | tf_op jit(solution)/shard_map/ppermute | solution.py:472
  133.2 24.4 %collective-permute-start.15 = (f32[128,1024]{1,0:T(8,128)S(1)}, f32[128,1024]{1,0:T(8,128)S(1)}, u32[]{:S(2)}, u32[]{:S(2)}) collective-permute-start(f32[128,1024]{1,0:T(8,128)S(1)} %copy-done.3), channel_id=1, source_target_pairs={{0,96},{16,112},{32,0},{48,16},{64,32},{80,48},{96,64},{112,80},{1... | collective-permute-start | bytes 1572872 | tf_op jit(solution)/shard_map/ppermute | solution.py:472
  157.8 35.8 %copy-start.2 = (f32[4,128,1024]{2,1,0:T(8,128)}, f32[4,128,1024]{2,1,0:T(8,128)S(1)}, u32[]{:S(2)}) copy-start(f32[4,128,1024]{2,1,0:T(8,128)S(1)} %pad_maximum_fusion.own_ref) | copy-start | bytes 6291460
  157.8 35.8 %collective-permute-start.16 = (f32[4,128,1024]{2,1,0:T(8,128)S(1)}, f32[4,128,1024]{2,1,0:T(8,128)}, u32[]{:S(2)}, u32[]{:S(2)}) collective-permute-start(f32[4,128,1024]{2,1,0:T(8,128)S(1)} %pad_maximum_fusion.own_ref), channel_id=1, source_target_pairs={{0,16},{16,0},{32,48},{48,32},{64,80},{80,64},{96,112},{112,96},{1... | collective-permute-start | bytes 6291464 | tf_op jit(solution)/shard_map/ppermute | solution.py:478
  192.8 0.8 copy-start.1
Sparse Core Ops, SparseCore 0:
  14.0 43.6 reduce-scatter.1
  85.6 76.0 all-gather.1
where the time goes:
time: 225 us
  waiting for transfers between devices  81.1 us (36%)
  Pallas kernels  61.8 us (27%)
  starting transfers between devices  36.8 us (16%)
  blocking collectives  23.4 us (10%)
  between operations  14.3 us (6%)
  other arithmetic  4.02 us (2%)
  local copies, waits for them, and re-layouts  3.63 us (2%)
    pallas_call x1, Pallas kernels, chol(): pl.pallas_call(chol_kernel, grid_spec=pltpu.PrefetchScalarGridSpec(num_sc...  32.8 us
    pallas_call x1, Pallas kernels, finish(): pl.pallas_call(finish_kernel, grid_spec=pltpu.PrefetchScalarGridSpec(num_...  24.6 us
    ppermute x3, waiting for transfers between devices, per_device(): own.append(lax.ppermute(y, 'row', pairs))  24.1 us
    all_gather x1, blocking collectives, gathered_over_cols(): return lax.all_gather(d, 'col', axis=0, tiled=True)  23.4 us
    ppermute x2, waiting for transfers between devices, per_device(): recv.append(lax.ppermute(send[h], both, pairs))  21.2 us
    ppermute x3, waiting for transfers between devices, over_rows_of_devices(): parts.append(lax.ppermute(d, 'row', pairs))  14.5 us
    ppermute x7, starting transfers between devices, diagonal(): recv.append(lax.ppermute(chunks[s], 'row', pairs))  13.7 us
    reduce_scatter x1, waiting for transfers between devices, per_device(): y = lax.psum_scatter(x, 'row', scatter_dimension=0, tiled=True)  10.2 us
  transfers between devices with their start and end apart: 20, of which 13 were waited for; matrix products, arithmetic and copies ran while one was open for 1% of the time, Pallas kernels for 15%

commit v1 on v0

--- a/solution.py
+++ b/solution.py
@@ -246,13 +246,18 @@
                 jnp.concatenate([top, low], 0)
             )
 
-    def solve(b_ref, hi_ref, lo_ref, base, slot, at, size):
+    def solve(b_ref, hi_ref, lo_ref, base, slot, at, size, turn):
         cols = pl.ds(at, size)
-        for b in range(n // wide):
+        count = n // wide
+
+        def given(b):
+            return b_ref[pl.ds(pl.multiple_of(lax.rem(turn + b, count) * wide, wide), wide), cols]
+
+        for b in range(count):
             own = slice(b * wide, b * wide + wide)
             rest = slice(b * wide + wide, n)
-            src = rest_ref if b else b_ref
-            sol = split2(prod3((wh[own, :], wl[own, :]), split2(src[own, cols]), 1, 0))
+            rhs = rest_ref[own, cols] if b else given(0)
+            sol = split2(prod3((wh[own, :], wl[own, :]), split2(rhs), 1, 0))
             for ref, x in zip((hi_ref, lo_ref), sol):
                 for e in range(size // width):
                     keep = flag_ref[base + slot + e, b * wide // width] > 0
@@ -260,29 +265,33 @@
                     where = pl.ds(pl.multiple_of((slot + e) * width, width), width)
                     ref[own, where] = jnp.where(keep, piece, jnp.zeros_like(piece))
             if rest.start < n:
-                rest_ref[rest, cols] = src[rest, cols] - prod3((uh[own, rest], ul[own, rest]), sol, 0, 0)
-
-    def solve_pair(b_ref, hi_ref, lo_ref, base, slot):
+                less = prod3((uh[own, rest], ul[own, rest]), sol, 0, 0)
+                for e in range(b + 1, count):
+                    rows = slice(e * wide, e * wide + wide)
+                    before = rest_ref[rows, cols] if b else given(e)
+                    rest_ref[rows, cols] = before - less[rows.start - rest.start : rows.stop - rest.start]
+
+    def solve_pair(b_ref, hi_ref, lo_ref, base, slot, turn):
         first, second = flag_ref[base + slot, 0], flag_ref[base + slot + 1, 0]
 
         @pl.when(first + second == 2)
         def _():
-            solve(b_ref, hi_ref, lo_ref, base, slot, 0, 2 * width)
+            solve(b_ref, hi_ref, lo_ref, base, slot, 0, 2 * width, turn)
 
         @pl.when(first + second == 1)
         def _():
             at = pl.multiple_of(second * width, width)
-            solve(b_ref, hi_ref, lo_ref, base, slot + second, at, width)
+            solve(b_ref, hi_ref, lo_ref, base, slot + second, at, width, turn)
 
     @pl.when(step < 2)
     def _():
-        solve_pair(r_ref, rh, rl, 0, 2 * step)
+        solve_pair(r_ref, rh, rl, 0, 2 * step, lax.div(q, 4) + 2 * step)
 
     @pl.when(step == 2)
     def _():
         for s in range(8):
             slab_copy(s).wait()
-        solve_pair(c_ref, ch, cl, 4, 0)
+        solve_pair(c_ref, ch, cl, 4, 0, 0)
 
     @pl.when(step >= 3)
     def _():
@@ -458,7 +467,8 @@
         for r in range(rows_dev):
             for s in range(cols_dev):
                 flip = h if s < rows_dev else 1 - h
-                pairs.append((r * cols_dev + s, (s % rows_dev) * cols_dev + 2 * r + flip))
+                to = (r // 2 + s // 4) % 4 * 4 + 2 * (r % 2) + flip
+                pairs.append((r * cols_dev + s, (s % rows_dev) * cols_dev + to))
         recv.append(lax.ppermute(send[h], both, pairs))
 
     even = c % 2 == 0

time: 225 us -> 219 us (0.973)
  waiting for transfers between devices: 81.1 us -> 76.7 us
    ppermute x2, waiting for transfers between devices: 21.2 us -> 14.4 us  [per_device(): recv.append(lax.ppermute(send[h], both, pairs))]
    ppermute x1, starting transfers between devices: 4.71 us -> 2.22 us  [over_rows_of_devices(): partner = lax.ppermute(mine, 'row', [(r, r ^ 1) for r in range(rows_dev)])]
    ppermute x3, waiting for transfers between devices: 14.5 us -> 17 us  [over_rows_of_devices(): parts.append(lax.ppermute(d, 'row', pairs))]
where the time goes in v1:
time: 219 us; the launch traced here: 218 us
  waiting for transfers between devices  76.7 us (35%)
  Pallas kernels  61.8 us (28%)
  starting transfers between devices  35.5 us (16%)
  blocking collectives  22.1 us (10%)
  between operations  14.4 us (7%)
  other arithmetic  4.02 us (2%)
  local copies, waits for them, and re-layouts  3.63 us (2%)
    pallas_call x1, Pallas kernels, chol(): pl.pallas_call(chol_kernel, grid_spec=pltpu.PrefetchScalarGridSpec(num_sc...  32.8 us
    pallas_call x1, Pallas kernels, finish(): pl.pallas_call(finish_kernel, grid_spec=pltpu.PrefetchScalarGridSpec(num_...  24.6 us
    ppermute x3, waiting for transfers between devices, per_device(): own.append(lax.ppermute(y, 'row', pairs))  24 us
    all_gather x1, blocking collectives, gathered_over_cols(): return lax.all_gather(d, 'col', axis=0, tiled=True)  22.1 us
    ppermute x3, waiting for transfers between devices, over_rows_of_devices(): parts.append(lax.ppermute(d, 'row', pairs))  17 us
    ppermute x2, waiting for transfers between devices, per_device(): recv.append(lax.ppermute(send[h], both, pairs))  14.4 us
    ppermute x7, starting transfers between devices, diagonal(): recv.append(lax.ppermute(chunks[s], 'row', pairs))  13.7 us
    reduce_scatter x1, waiting for transfers between devices, per_device(): y = lax.psum_scatter(x, 'row', scatter_dimension=0, tiled=True)  10.2 us
  transfers between devices with their start and end apart: 20, of which 13 were waited for; matrix products, arithmetic and copies ran while one was open for 1% of the time, Pallas kernels for 15%

profile of v1, /device:TPU:31, one launch (start us, length us, event | category | flops | bytes accessed | tf_op | source)
XLA Modules:
  0.0 218.1 jit_solution(10073812942282955852)
XLA Ops:
  6.5 0.0 reduce-scatter.2.cloned.1.call-start
  7.3 0.1 stack.92.at_ref
  7.4 4.4 %strips.1 = (f32[1024,1024]{1,0:T(8,128)S(1)}, f32[64,512]{1,0:T(8,128)S(1)}, f32[64,512]{1,0:T(8,128)S(1)}, f32[64,512]{1,0:T(8,128)S(1)}, f32[64,512]{1,0:T(8,...) custom-call(s32[7]{0:T(128)S(1)} %stack.92.at_ref, ...), custom_call_target="tpu_custom_call" | custom-call | tf_op jit(solution)/shard_map/strips/pallas_call | solution.py:193
  11.8 0.0 copy-start
  11.9 2.0 copy-done
  13.9 0.0 reduce-scatter.2.cloned.1.call-update
  13.9 0.7 collective-permute-start
  14.6 0.5 collective-permute-start.1
  15.0 0.4 collective-permute-start.2
  15.4 3.3 %collective-permute-start.3 = (f32[64,512]{1,0:T(8,128)S(1)}, f32[64,512]{1,0:T(8,128)S(1)}, u32[]{:S(2)}, u32[]{:S(2)}) collective-permute-start(f32[64,512]{1,0:T(8,128)S(1)} %get-tuple-element.25), channel_id=1, source_target_pairs={{0,64},{16,80},{32,96},{48,112},{64,0},{80,16},{96,32},{112,48},{1... | collective-permute-start | bytes 393224 | tf_op jit(solution)/shard_map/ppermute | solution.py:394
  18.8 0.4 collective-permute-start.4
  19.2 1.6 collective-permute-done
  20.8 0.3 collective-permute-start.5
  21.1 0.2 collective-permute-done.1
  21.3 8.0 %collective-permute-start.6 = (f32[64,512]{1,0:T(8,128)S(1)}, f32[64,512]{1,0:T(8,128)S(1)}, u32[]{:S(2)}, u32[]{:S(2)}) collective-permute-start(f32[64,512]{1,0:T(8,128)S(1)} %get-tuple-element.28), channel_id=1, source_target_pairs={{0,16},{16,32},{32,48},{48,64},{64,80},{80,96},{96,112},{112,0},{1... | collective-permute-start | bytes 393224 | tf_op jit(solution)/shard_map/ppermute | solution.py:394
  29.3 0.0 collective-permute-done.2
  29.3 0.0 collective-permute-done.3
  29.3 0.0 collective-permute-done.4
  29.3 0.1 collective-permute-done.5
  29.4 3.8 %collective-permute-done.6 = f32[64,512]{1,0:T(8,128)S(1)} collective-permute-done((f32[64,512]{1,0:T(8,128)S(1)}, f32[64,512]{1,0:T(8,128)S(1)}, u32[]{:S(2)}, u32[]{:S(2)}) %collective-permute-start.6) | collective-permute-done | bytes 131104 | tf_op jit(solution)/shard_map/ppermute | solution.py:394
  33.2 0.1 select_select_fusion.1
  33.3 0.1 select_select_fusion
  33.4 0.7 copy.12
  34.1 7.8 %all-to-all-start = ((f32[16,2,8,256]{3,2,1,0:T(8,128)}), f32[16,2,8,256]{3,2,1,0:T(8,128)S(1)}, u32[]{:S(2)}, u32[]{:S(2)}) async-start(f32[16,2,8,256]{3,2,1,0:T(8,128)} %bitcast.16), calls=%async_computation | async-start | bytes 524288 | tf_op jit(solution)/shard_map/all_to_all | solution.py:402
  42.0 0.0 all-gather.2.cloned.1.call-start
  42.0 5.5 %all-to-all-done = f32[16,2,8,256]{3,2,1,0:T(8,128)S(1)} async-done(((f32[16,2,8,256]{3,2,1,0:T(8,128)}), f32[16,2,8,256]{3,2,1,0:T(8,128)S(1)}, u32[]{:S(2)}, u32[]{:S(2)}) %all-to-all-start) | async-done | bytes 262176 | tf_op jit(solution)/shard_map/all_to_all | solution.py:402
  47.5 10.2 %reduce-scatter.2.cloned.1.call-done = f32[128,1024]{1,0:T(8,128)} async-done(((f32[1024,1024]{1,0:T(8,128)}), f32[128,1024]{1,0:T(8,128)}) %reduce-scatter.2.cloned.1.call-update) | async-done | bytes 524304 | tf_op jit(solution)/shard_map/reduce_scatter | solution.py:452
  57.7 1.1 slice_select_fusion.1
  58.8 3.4 %collective-permute-start.7 = (f32[64,1024]{1,0:T(8,128)S(1)}, f32[64,1024]{1,0:T(8,128)S(1)}, u32[]{:S(2)}, u32[]{:S(2)}) collective-permute-start(f32[64,1024]{1,0:T(8,128)S(1)} %get-tuple-element.41), channel_id=1, source_target_pairs={{0,0},{1,16},{2,32},{3,48},{4,68},{5,84},{6,100},{7,116},{8,9},{9,... | collective-permute-start | bytes 786440 | tf_op jit(solution)/shard_map/ppermute | solution.py:472
  62.1 2.4 %collective-permute-start.8 = (f32[64,1024]{1,0:T(8,128)S(1)}, f32[64,1024]{1,0:T(8,128)S(1)}, u32[]{:S(2)}, u32[]{:S(2)}) collective-permute-start(f32[64,1024]{1,0:T(8,128)S(1)} %get-tuple-element.42), channel_id=1, source_target_pairs={{0,1},{1,17},{2,33},{3,49},{4,69},{5,85},{6,101},{7,117},{8,8},{9,... | collective-permute-start | bytes 786440 | tf_op jit(solution)/shard_map/ppermute | solution.py:472
  64.5 8.7 %collective-permute-done.7 = f32[64,1024]{1,0:T(8,128)S(1)} collective-permute-done((f32[64,1024]{1,0:T(8,128)S(1)}, f32[64,1024]{1,0:T(8,128)S(1)}, u32[]{:S(2)}, u32[]{:S(2)}) %collective-permute-start.7) | collective-permute-done | bytes 262176 | tf_op jit(solution)/shard_map/ppermute | solution.py:472
  73.2 5.7 %collective-permute-done.8 = f32[64,1024]{1,0:T(8,128)S(1)} collective-permute-done((f32[64,1024]{1,0:T(8,128)S(1)}, f32[64,1024]{1,0:T(8,128)S(1)}, u32[]{:S(2)}, u32[]{:S(2)}) %collective-permute-start.8) | collective-permute-done | bytes 262176 | tf_op jit(solution)/shard_map/ppermute | solution.py:472
  79.0 0.8 pad_maximum_fusion.2
  79.8 0.0 all-gather.2.cloned.1.call-update
  79.9 22.1 %all_gather.6 = f32[384,256]{1,0:T(8,128)S(1)} all-gather(f32[24,256]{1,0:T(8,128)S(1)} %pad_maximum_fusion.3), channel_id=1, replica_groups=mesh['row'=8,'col'=16] {'col'}, dimensions={0}, use_global_device_ids=true | all-gather | bytes 417792 | tf_op jit(solution)/shard_map/all_gather | solution.py:414
  102.0 0.0 collective-permute-start.11
  102.0 0.3 collective-permute-start.10
  102.3 2.4 %collective-permute-start.9 = (f32[384,256]{1,0:T(8,128)S(1)}, f32[384,256]{1,0:T(8,128)S(1)}, u32[]{:S(2)}, u32[]{:S(2)}) collective-permute-start(f32[384,256]{1,0:T(8,128)S(1)} %all_gather.6), channel_id=1, source_target_pairs={{0,32},{16,48},{32,64},{48,80},{64,96},{80,112},{96,0},{112,16},{1... | collective-permute-start | bytes 1179656 | tf_op jit(solution)/shard_map/ppermute | solution.py:421
  104.7 16.3 %collective-permute-done.11 = f32[384,256]{1,0:T(8,128)S(1)} collective-permute-done((f32[384,256]{1,0:T(8,128)S(1)}, f32[384,256]{1,0:T(8,128)S(1)}, u32[]{:S(2)}, u32[]{:S(2)}) %collective-permute-start.11) | collective-permute-done | bytes 393248 | tf_op jit(solution)/shard_map/ppermute | solution.py:421
  121.0 0.0 collective-permute-done.10
  121.0 0.7 collective-permute-done.9
  121.7 0.1 pad_maximum_fusion.1.own_ref
  121.8 2.2 %collective-permute-start.12 = (f32[4,48,8,256]{3,2,1,0:T(8,128)S(1)}, f32[4,48,8,256]{3,2,1,0:T(8,128)S(1)}, u32[]{:S(2)}, u32[]{:S(2)}) collective-permute-start(f32[4,48,8,256]{3,2,1,0:T(8,128)S(1)} %pad_maximum_fusion.1.own_ref), channel_id=1, source_target_pairs={{0,16},{16,0},{32,48},{48,32},{64,80},{80,64},{96,112},{112,96},{1... | collective-permute-start | bytes 4718600 | tf_op jit(solution)/shard_map/ppermute | solution.py:423
  124.0 0.6 collective-permute-start.14
  124.6 1.7 collective-permute-start.13
  126.4 0.3 collective-permute-start.15
  126.6 12.3 %collective-permute-done.14 = f32[128,1024]{1,0:T(8,128)S(1)} collective-permute-done((f32[128,1024]{1,0:T(8,128)S(1)}, f32[128,1024]{1,0:T(8,128)S(1)}, u32[]{:S(2)}, u32[]{:S(2)}) %collective-permute-start.14) | collective-permute-done | bytes 524320 | tf_op jit(solution)/shard_map/ppermute | solution.py:482
  138.9 11.0 %collective-permute-done.13 = f32[128,1024]{1,0:T(8,128)S(1)} collective-permute-done((f32[128,1024]{1,0:T(8,128)S(1)}, f32[128,1024]{1,0:T(8,128)S(1)}, u32[]{:S(2)}, u32[]{:S(2)}) %collective-permute-start.13) | collective-permute-done | bytes 524320 | tf_op jit(solution)/shard_map/ppermute | solution.py:482
  149.9 0.8 collective-permute-done.15
  150.7 0.2 pad_maximum_fusion.own_ref
  150.9 0.0 copy-start.2
  150.9 0.0 collective-permute-done.12.near_ref
  150.9 0.6 collective-permute-start.16
  151.5 0.1 add_bitcast_fusion
  151.6 0.1 pad_add_fusion.1
  151.7 0.1 compare_convert_fusion
  151.8 0.1 compare_convert_fusion.1
  151.9 0.6 pad_add_fusion.flag_ref
  152.5 0.7 select_select_fusion.2.mode_ref
  153.1 32.8 %chol.1 = (f32[1024,1024]{1,0:T(8,128)}, f32[1024,128]{1,0:T(8,128)S(1)}) custom-call(s32[1]{0:T(128)} %bitcast.2.q_ref, f32[4,48,8,256]{3,2,1,0:T(8,128)S(1)} %pad_maximum_fusion.1.own_ref, f32[4,48,8,256]{3,2,1,0:T(8,128)S(1)} %collective-permute-done.12.near_ref), custom_call_target="tpu_custom_call" | custom-call | tf_op jit(solution)/shard_map/chol/pallas_call | solution.py:153
  185.9 0.8 copy-done.1
  186.7 0.0 collective-permute-done.16.other_ref
  186.7 0.0 copy-done.2
  186.7 24.6 %finish.1 = f32[16384,128]{1,0:T(8,128)} custom-call(s32[7,2]{1,0:T(8,128)} %pad_add_fusion.flag_ref, s32[4,2]{1,0:T(4,128)} %select_select_fusion.2.mode_ref, f32[1024,1024]{1,0:T(8,128)} %get-tuple-element.36.u_ref, f32[1024,128]{1,0:T(8,128)} %copy-done.1, f32[1024,2048]{1,0:T(8,128)} %all-gather.2.cloned.1.call-done.r_ref, f32[4,128,1024]{2,1,0:T(8,128)} %copy-done.2, ...), custom_call_target="tpu_custom_call" | custom-call | tf_op jit(solution)/shard_map/finish/pallas_call | solution.py:362
  (13 shorter events, 0.1 us)
Async XLA Ops:
  6.5 51.2 %reduce-scatter.2.cloned.1.call-start = ((), (), s32[]{:S(2)}) async-start(), calls=%async_computation.2 | async-start | bytes 4718592 | tf_op jit(solution)/shard_map/reduce_scatter | solution.py:452
  11.8 2.0 copy-start
  13.9 6.9 %collective-permute-start = (f32[64,512]{1,0:T(8,128)S(1)}, f32[64,512]{1,0:T(8,128)S(1)}, u32[]{:S(2)}, u32[]{:S(2)}) collective-permute-start(f32[64,512]{1,0:T(8,128)S(1)} %get-tuple-element.22), channel_id=1, source_target_pairs={{0,112},{16,0},{32,16},{48,32},{64,48},{80,64},{96,80},{112,96},{1... | collective-permute-start | bytes 393224 | tf_op jit(solution)/shard_map/ppermute | solution.py:394
  14.6 6.7 %collective-permute-start.1 = (f32[64,512]{1,0:T(8,128)S(1)}, f32[64,512]{1,0:T(8,128)S(1)}, u32[]{:S(2)}, u32[]{:S(2)}) collective-permute-start(f32[64,512]{1,0:T(8,128)S(1)} %get-tuple-element.23), channel_id=1, source_target_pairs={{0,96},{16,112},{32,0},{48,16},{64,32},{80,48},{96,64},{112,80},{1... | collective-permute-start | bytes 393224 | tf_op jit(solution)/shard_map/ppermute | solution.py:394
  15.0 14.3 %collective-permute-start.2 = (f32[64,512]{1,0:T(8,128)S(1)}, f32[64,512]{1,0:T(8,128)S(1)}, u32[]{:S(2)}, u32[]{:S(2)}) collective-permute-start(f32[64,512]{1,0:T(8,128)S(1)} %get-tuple-element.24), channel_id=1, source_target_pairs={{0,80},{16,96},{32,112},{48,0},{64,16},{80,32},{96,48},{112,64},{1... | collective-permute-start | bytes 393224 | tf_op jit(solution)/shard_map/ppermute | solution.py:394
  15.4 13.9 %collective-permute-start.3 = (f32[64,512]{1,0:T(8,128)S(1)}, f32[64,512]{1,0:T(8,128)S(1)}, u32[]{:S(2)}, u32[]{:S(2)}) collective-permute-start(f32[64,512]{1,0:T(8,128)S(1)} %get-tuple-element.25), channel_id=1, source_target_pairs={{0,64},{16,80},{32,96},{48,112},{64,0},{80,16},{96,32},{112,48},{1... | collective-permute-start | bytes 393224 | tf_op jit(solution)/shard_map/ppermute | solution.py:394
  18.8 10.5 %collective-permute-start.4 = (f32[64,512]{1,0:T(8,128)S(1)}, f32[64,512]{1,0:T(8,128)S(1)}, u32[]{:S(2)}, u32[]{:S(2)}) collective-permute-start(f32[64,512]{1,0:T(8,128)S(1)} %get-tuple-element.26), channel_id=1, source_target_pairs={{0,48},{16,64},{32,80},{48,96},{64,112},{80,0},{96,16},{112,32},{1... | collective-permute-start | bytes 393224 | tf_op jit(solution)/shard_map/ppermute | solution.py:394
  20.8 8.6 %collective-permute-start.5 = (f32[64,512]{1,0:T(8,128)S(1)}, f32[64,512]{1,0:T(8,128)S(1)}, u32[]{:S(2)}, u32[]{:S(2)}) collective-permute-start(f32[64,512]{1,0:T(8,128)S(1)} %get-tuple-element.27), channel_id=1, source_target_pairs={{0,32},{16,48},{32,64},{48,80},{64,96},{80,112},{96,0},{112,16},{1... | collective-permute-start | bytes 393224 | tf_op jit(solution)/shard_map/ppermute | solution.py:394
  21.3 11.9 %collective-permute-start.6 = (f32[64,512]{1,0:T(8,128)S(1)}, f32[64,512]{1,0:T(8,128)S(1)}, u32[]{:S(2)}, u32[]{:S(2)}) collective-permute-start(f32[64,512]{1,0:T(8,128)S(1)} %get-tuple-element.28), channel_id=1, source_target_pairs={{0,16},{16,32},{32,48},{48,64},{64,80},{80,96},{96,112},{112,0},{1... | collective-permute-start | bytes 393224 | tf_op jit(solution)/shard_map/ppermute | solution.py:394
  34.1 13.4 %all-to-all-start = ((f32[16,2,8,256]{3,2,1,0:T(8,128)}), f32[16,2,8,256]{3,2,1,0:T(8,128)S(1)}, u32[]{:S(2)}, u32[]{:S(2)}) async-start(f32[16,2,8,256]{3,2,1,0:T(8,128)} %bitcast.16), calls=%async_computation | async-start | bytes 524288 | tf_op jit(solution)/shard_map/all_to_all | solution.py:402
  42.0 144.7 %all-gather.2.cloned.1.call-start = ((), (), s32[]{:S(2)}) async-start(), calls=%async_computation.3 | async-start | bytes 8912896 | tf_op jit(solution)/shard_map/all_gather | solution.py:478
  58.8 14.5 %collective-permute-start.7 = (f32[64,1024]{1,0:T(8,128)S(1)}, f32[64,1024]{1,0:T(8,128)S(1)}, u32[]{:S(2)}, u32[]{:S(2)}) collective-permute-start(f32[64,1024]{1,0:T(8,128)S(1)} %get-tuple-element.41), channel_id=1, source_target_pairs={{0,0},{1,16},{2,32},{3,48},{4,68},{5,84},{6,100},{7,116},{8,9},{9,... | collective-permute-start | bytes 786440 | tf_op jit(solution)/shard_map/ppermute | solution.py:472
  62.1 16.8 %collective-permute-start.8 = (f32[64,1024]{1,0:T(8,128)S(1)}, f32[64,1024]{1,0:T(8,128)S(1)}, u32[]{:S(2)}, u32[]{:S(2)}) collective-permute-start(f32[64,1024]{1,0:T(8,128)S(1)} %get-tuple-element.42), channel_id=1, source_target_pairs={{0,1},{1,17},{2,33},{3,49},{4,69},{5,85},{6,101},{7,117},{8,8},{9,... | collective-permute-start | bytes 786440 | tf_op jit(solution)/shard_map/ppermute | solution.py:472
  79.8 44.2 %copy-start.3 = (f32[128,1024]{1,0:T(8,128)S(1)}, f32[128,1024]{1,0:T(8,128)}, u32[]{:S(2)}) copy-start(f32[128,1024]{1,0:T(8,128)} %reduce-scatter.2.cloned.1.call-done) | copy-start | bytes 1572868
  102.0 19.0 %collective-permute-start.11 = (f32[384,256]{1,0:T(8,128)S(1)}, f32[384,256]{1,0:T(8,128)S(1)}, u32[]{:S(2)}, u32[]{:S(2)}) collective-permute-start(f32[384,256]{1,0:T(8,128)S(1)} %all_gather.6), channel_id=1, source_target_pairs={{0,96},{16,112},{32,0},{48,16},{64,32},{80,48},{96,64},{112,80},{1... | collective-permute-start | bytes 1179656 | tf_op jit(solution)/shard_map/ppermute | solution.py:421
  102.0 19.0 %collective-permute-start.10 = (f32[384,256]{1,0:T(8,128)S(1)}, f32[384,256]{1,0:T(8,128)S(1)}, u32[]{:S(2)}, u32[]{:S(2)}) collective-permute-start(f32[384,256]{1,0:T(8,128)S(1)} %all_gather.6), channel_id=1, source_target_pairs={{0,64},{16,80},{32,96},{48,112},{64,0},{80,16},{96,32},{112,48},{1... | collective-permute-start | bytes 1179656 | tf_op jit(solution)/shard_map/ppermute | solution.py:421
  102.3 19.4 %collective-permute-start.9 = (f32[384,256]{1,0:T(8,128)S(1)}, f32[384,256]{1,0:T(8,128)S(1)}, u32[]{:S(2)}, u32[]{:S(2)}) collective-permute-start(f32[384,256]{1,0:T(8,128)S(1)} %all_gather.6), channel_id=1, source_target_pairs={{0,32},{16,48},{32,64},{48,80},{64,96},{80,112},{96,0},{112,16},{1... | collective-permute-start | bytes 1179656 | tf_op jit(solution)/shard_map/ppermute | solution.py:421
  121.8 29.1 %collective-permute-start.12 = (f32[4,48,8,256]{3,2,1,0:T(8,128)S(1)}, f32[4,48,8,256]{3,2,1,0:T(8,128)S(1)}, u32[]{:S(2)}, u32[]{:S(2)}) collective-permute-start(f32[4,48,8,256]{3,2,1,0:T(8,128)S(1)} %pad_maximum_fusion.1.own_ref), channel_id=1, source_target_pairs={{0,16},{16,0},{32,48},{48,32},{64,80},{80,64},{96,112},{112,96},{1... | collective-permute-start | bytes 4718600 | tf_op jit(solution)/shard_map/ppermute | solution.py:423
  124.0 14.9 %collective-permute-start.14 = (f32[128,1024]{1,0:T(8,128)S(1)}, f32[128,1024]{1,0:T(8,128)S(1)}, u32[]{:S(2)}, u32[]{:S(2)}) collective-permute-start(f32[128,1024]{1,0:T(8,128)S(1)} %copy-done.3), channel_id=1, source_target_pairs={{0,64},{16,80},{32,96},{48,112},{64,0},{80,16},{96,32},{112,48},{1... | collective-permute-start | bytes 1572872 | tf_op jit(solution)/shard_map/ppermute | solution.py:482
  124.6 25.3 %collective-permute-start.13 = (f32[128,1024]{1,0:T(8,128)S(1)}, f32[128,1024]{1,0:T(8,128)S(1)}, u32[]{:S(2)}, u32[]{:S(2)}) collective-permute-start(f32[128,1024]{1,0:T(8,128)S(1)} %copy-done.3), channel_id=1, source_target_pairs={{0,32},{16,48},{32,64},{48,80},{64,96},{80,112},{96,0},{112,16},{1... | collective-permute-start | bytes 1572872 | tf_op jit(solution)/shard_map/ppermute | solution.py:482
  126.4 24.3 %collective-permute-start.15 = (f32[128,1024]{1,0:T(8,128)S(1)}, f32[128,1024]{1,0:T(8,128)S(1)}, u32[]{:S(2)}, u32[]{:S(2)}) collective-permute-start(f32[128,1024]{1,0:T(8,128)S(1)} %copy-done.3), channel_id=1, source_target_pairs={{0,96},{16,112},{32,0},{48,16},{64,32},{80,48},{96,64},{112,80},{1... | collective-permute-start | bytes 1572872 | tf_op jit(solution)/shard_map/ppermute | solution.py:482
  150.9 35.8 %copy-start.2 = (f32[4,128,1024]{2,1,0:T(8,128)}, f32[4,128,1024]{2,1,0:T(8,128)S(1)}, u32[]{:S(2)}) copy-start(f32[4,128,1024]{2,1,0:T(8,128)S(1)} %pad_maximum_fusion.own_ref) | copy-start | bytes 6291460
  150.9 35.8 %collective-permute-start.16 = (f32[4,128,1024]{2,1,0:T(8,128)S(1)}, f32[4,128,1024]{2,1,0:T(8,128)}, u32[]{:S(2)}, u32[]{:S(2)}) collective-permute-start(f32[4,128,1024]{2,1,0:T(8,128)S(1)} %pad_maximum_fusion.own_ref), channel_id=1, source_target_pairs={{0,16},{16,0},{32,48},{48,32},{64,80},{80,64},{96,112},{112,96},{1... | collective-permute-start | bytes 6291464 | tf_op jit(solution)/shard_map/ppermute | solution.py:488
  185.9 0.8 copy-start.1
Sparse Core Ops, SparseCore 0:
  14.0 43.6 reduce-scatter.1
  80.0 71.5 all-gather.1
